TPU v7x, 32 devices: a whole 2x2x4 slice. The times are simulated.
32 devices in a mesh: dp: 4 (over y, core), row: 2 (over x), col: 4 (over z).
Axes of the slice: x: 2, y: 2, z: 4, core: 2. Of those that a mesh axis runs over, the one named last changes fastest.
Arguments:
- images: bfloat16 [4, 64, 32, 1024], P('dp', None, 'row', 'col'), may hold values from -6 to 6
- first_kernel: bfloat16 [64, 64, 3, 3], replicated, may hold values from -0.25 to 0.25
- second_kernel: bfloat16 [64, 64, 3, 3], replicated, may hold values from -0.25 to 0.25
- cotangent: bfloat16 [4, 64, 32, 1024], P('dp', None, 'row', 'col'), may hold values from -6 to 6
Outputs:
- outputs: bfloat16 [4, 64, 32, 1024], P('dp', None, 'row', 'col')
- input_grad: bfloat16 [4, 64, 32, 1024], P('dp', None, 'row', 'col')
- first_grad: float32 [64, 64, 3, 3], replicated
- second_grad: float32 [64, 64, 3, 3], replicated
All inputs are finite; a program needn't handle non-finite values.
Results may differ from a plain program's by a relative error of at most 0.005.
Values may be sent and summed in bfloat16 or wider, within the bound.
No kernel may reach another device: no remote copies, remote signals or barrier semaphores. Data moves between devices by JAX's collectives and lax.ppermute only.
A program may use at most 64 MiB of HBM per device.

v0:
```python
import math
import jax
import jax.numpy as jnp
from jax import lax
from jax.sharding import PartitionSpec as P


def extended(array, sides, width):
    for axis, dim in sides:
        size, length = (lax.axis_size(axis), array.shape[dim])
        up = [(i, (i + 1) % size) for i in range(size - 1)]
        down = [(j, i) for i, j in up]
        last = lax.slice_in_dim(array, length - width, length, axis=dim)
        leading = lax.slice_in_dim(array, 0, width, axis=dim)
        before = lax.ppermute(last, axis, up)
        after = lax.ppermute(leading, axis, down)
        array = jnp.concatenate([before, array, after], axis=dim)
    return array


def convolve(padded, kernel):
    return lax.conv_general_dilated(
        padded,
        kernel,
        (1, 1),
        "VALID",
        dimension_numbers=("NCHW", "OIHW", "NCHW"),
        preferred_element_type=jnp.float32,
    )


def flipped(kernel):
    return jnp.flip(kernel, (2, 3)).transpose(1, 0, 2, 3)


def silu_grad(value):
    sigma = jax.nn.sigmoid(value)
    return sigma * (1.0 + value * (1.0 - sigma))


def kernel_grad(padded, upstream):
    height = upstream.shape[2]
    breadth = upstream.shape[3]
    outer = []
    for offset_row in range(3):
        inner = []
        for offset_col in range(3):
            window = padded[
                :, :, offset_row : offset_row + height, offset_col : offset_col + breadth
            ]
            inner.append(
                jnp.einsum("nihw,nohw->oi", window, upstream, preferred_element_type=jnp.float32)
            )
        outer.append(jnp.stack(inner, -1))
    return jnp.stack(outer, 2)


def grid_mask(height, breadth):
    row_index = lax.axis_index("row") * height + jnp.arange(height + 2, dtype=jnp.int32) - 1
    col_index = lax.axis_index("col") * breadth + jnp.arange(breadth + 2, dtype=jnp.int32) - 1
    row_valid = (row_index >= 0) & (row_index < height * lax.axis_size("row"))
    col_valid = (col_index >= 0) & (col_index < breadth * lax.axis_size("col"))
    return (row_valid[:, None] & col_valid[None, :]).astype(jnp.float32)


def on_device(images, first_kernel, second_kernel, cotangent):
    channels = images.shape[1]
    height = images.shape[2]
    breadth = images.shape[3]
    total_pixels = (
        images.shape[0]
        * height
        * breadth
        * lax.axis_size("dp")
        * lax.axis_size("row")
        * lax.axis_size("col")
    )
    factor = 1.0 / math.sqrt(total_pixels)
    stacked = jnp.concatenate((images, cotangent), axis=1)
    both = extended(stacked, (("row", 2), ("col", 3)), 2)
    widened = both[:, :channels]
    widened_cot = both[:, channels:]
    inside = grid_mask(height, breadth)
    hidden = convolve(widened, first_kernel)
    act_padded = (jax.nn.silu(hidden) * inside).astype(jnp.bfloat16)
    padded_in = widened[:, :, 1:-1, 1:-1]
    outputs = convolve(act_padded, second_kernel).astype(jnp.bfloat16)
    second_grad = kernel_grad(act_padded, cotangent)
    act_grad = convolve(widened_cot, flipped(second_kernel))
    hid_padded = (act_grad * silu_grad(hidden) * inside).astype(jnp.bfloat16)
    hid_grad = hid_padded[:, :, 1:-1, 1:-1]
    input_grad = convolve(hid_padded, flipped(first_kernel)).astype(jnp.bfloat16)
    first_grad = kernel_grad(padded_in, hid_grad)
    first_grad, second_grad = lax.psum((first_grad, second_grad), ("dp", "row", "col"))
    return (outputs, input_grad, first_grad * factor, second_grad * factor)


def solution(mesh):
    in_specs = (P("dp", None, "row", "col"), P(), P(), P("dp", None, "row", "col"))
    out_specs = (P("dp", None, "row", "col"), P("dp", None, "row", "col"), P(), P())
    return jax.shard_map(
        on_device, mesh=mesh, in_specs=in_specs, out_specs=out_specs, check_vma=False
    )
```

profile of v0, /device:TPU:0, one launch (start us, length us, event | category | flops | bytes accessed | tf_op | source)
XLA Modules:
  0.0 264.4 jit_solution(4958273212836746187)
XLA Ops:
  7.2 1.2 copy_dynamic-update-slice_fusion.1
  8.5 1.2 copy_dynamic-update-slice_fusion
  9.7 4.9 %collective-permute-start = (bf16[1,128,2,256]{3,1,2,0:T(8,128)(2,1)S(1)}, bf16[1,128,2,256]{3,1,2,0:T(8,128)(2,1)S(1)}, u32[]{:S(2)}, u32[]{:S(2)}) collective-permute-start(bf16[1,128,2,256]{3,1,2,0:T(8,128)(2,1)S(1)} %get-tuple-element.22), channel_id=1, source_target_pairs={{0,4},{1,5},{2,6},{3,7},{8,12},{9,13},{10,14},{11,15},{16,20},{17,... | collective-permute-start | bytes 393224 | tf_op jit(solution)/shard_map/ppermute | solution.py:15
  14.6 1.3 collective-permute-start.1
  15.9 1.4 collective-permute-done
  17.3 4.1 %collective-permute-done.1 = bf16[1,128,2,256]{3,1,2,0:T(8,128)(2,1)S(1)} collective-permute-done((bf16[1,128,2,256]{3,1,2,0:T(8,128)(2,1)S(1)}, bf16[1,128,2,256]{3,1,2,0:T(8,128)(2,1)S(1)}, u32[]{:S(2)}, u32[]{:S(2)}) %collective-permute-start.1) | collective-permute-done | bytes 131104 | tf_op jit(solution)/shard_map/ppermute | solution.py:16
  21.6 0.3 fusion.118
  22.0 0.3 copy.72
  22.2 3.5 %collective-permute-start.2 = (bf16[1,128,20,2]{1,3,2,0:T(2,128)(2,1)S(1)}, bf16[1,128,20,2]{1,3,2,0:T(2,128)(2,1)S(1)}, u32[]{:S(2)}, u32[]{:S(2)}) collective-permute-start(bf16[1,128,20,2]{1,3,2,0:T(2,128)(2,1)S(1)} %copy.72), channel_id=1, source_target_pairs={{0,1},{1,2},{2,3},{4,5},{5,6},{6,7},{8,9},{9,10},{10,11},{12,13},{... | collective-permute-start | bytes 30728 | tf_op jit(solution)/shard_map/ppermute | solution.py:15
  26.0 1.3 collective-permute-start.3
  27.4 0.4 copy.74
  27.8 3.8 %collective-permute-done.3 = bf16[1,128,20,2]{1,3,2,0:T(2,128)(2,1)S(1)} collective-permute-done((bf16[1,128,20,2]{1,3,2,0:T(2,128)(2,1)S(1)}, bf16[1,128,20,2]{1,3,2,0:T(2,128)(2,1)S(1)}, u32[]{:S(2)}, u32[]{:S(2)}) %collective-permute-start.3) | collective-permute-done | bytes 10272 | tf_op jit(solution)/shard_map/ppermute | solution.py:16
  31.6 0.4 copy.75
  32.0 0.9 copy-done.5
  32.9 1.2 pad_maximum_fusion
  34.4 3.5 %reshape.214 = bf16[64,20,1,8,33]{4,3,0,1,2:T(8,128)(2,1)} reshape(bf16[64,20,1,264]{3,0,1,2:T(8,128)(2,1)S(1)} %pad) | data formatting | bytes 1351680 | tf_op jit(solution)/shard_map/conv_general_dilated | solution.py:22
  37.9 4.6 %copy.78 = bf16[64,20,1,8,33]{0,3,4,1,2:T(8,128)(2,1)} copy(bf16[64,20,1,8,33]{4,3,0,1,2:T(8,128)(2,1)} %reshape.214) | data formatting | bytes 1351680 | tf_op jit(solution)/shard_map/conv_general_dilated | solution.py:22
  42.5 0.9 slice.133
  43.6 3.3 %reshape.216 = bf16[64,20,1,8,33]{4,3,0,1,2:T(8,128)(2,1)} reshape(bf16[64,20,1,264]{3,0,1,2:T(8,128)(2,1)S(1)} %pad.4) | data formatting | bytes 1351680 | tf_op jit(solution)/shard_map/conv_general_dilated | solution.py:22
  46.9 4.7 %copy.87 = bf16[64,20,1,8,33]{0,3,4,1,2:T(8,128)(2,1)} copy(bf16[64,20,1,8,33]{4,3,0,1,2:T(8,128)(2,1)} %reshape.216) | data formatting | bytes 1351680 | tf_op jit(solution)/shard_map/conv_general_dilated | solution.py:22
  51.6 0.9 slice.138
  52.5 4.5 %fusion.4 = (f32[18,8,33,64]{3,1,2,0:T(8,128)}, f32[18,8,33,64]{3,1,2,0:T(8,128)S(1)}) fusion(pred[8,33]{0,1:T(8,128)(4,1)S(1)} %copy-done.25, bf16[64,64,3,3]{1,0,3,2:T(8,128)(2,1)S(1)} %copy-done, bf16[64,20,1,7,2]{0,3,4,1,2:T(8,128)(2,1)S(1)} %slice.133, bf16[64,20,1,8,33]{0,3,4,1,2:T(8,128)(2,1)S(1)} %copy-done.7), kind=kOutput, calls=%fused_computation.8 | convolution fusion | flops 354026496 | bytes 3218696 | tf_op jit(solution)/shard_map/conv_general_dilated | solution.py:22
  57.0 3.7 %select_multiply_fusion = f32[18,8,33,64]{3,1,2,0:T(8,128)} fusion(f32[18,8,33,64]{3,1,2,0:T(8,128)S(1)} %get-tuple-element.27, bf16[64,64,3,3]{1,0,3,2:T(8,128)(2,1)S(1)} %copy-done.24, bf16[64,20,1,7,2]{0,3,4,1,2:T(8,128)(2,1)S(1)} %slice.138, bf16[64,20,1,8,33]{0,3,4,1,2:T(8,128)(2,1)S(1)} %copy-done.8, pred[8,33]{0,1:T(8,128)(4,1)S(1)} %copy-done.25), kind=kOutput, calls=%fused_computation.6 | convolution fusion | flops 355547136 | bytes 3218696 | tf_op jit(solution)/shard_map/conv_general_dilated | solution.py:22
  60.8 5.2 %copy.127 = f32[18,8,33,64]{2,1,3,0:T(8,128)} copy(f32[18,8,33,64]{3,1,2,0:T(8,128)} %select_multiply_fusion) | data formatting | bytes 2433024 | tf_op jit(solution)/shard_map/mul | solution.py:90
  65.9 3.9 %reshape.213 = f32[18,1,264,64]{2,3,0,1:T(8,128)S(1)} reshape(f32[18,8,33,64]{2,1,3,0:T(8,128)} %copy.127) | data formatting | bytes 2433024 | tf_op jit(solution)/shard_map/mul | solution.py:90
  69.8 5.1 %copy.126 = f32[18,8,33,64]{2,1,3,0:T(8,128)} copy(f32[18,8,33,64]{3,1,2,0:T(8,128)} %get-tuple-element.26) | data formatting | bytes 2433024 | tf_op jit(solution)/shard_map/jit(silu)/mul | solution.py:85
  74.9 5.0 %reshape.212 = f32[18,1,264,64]{2,3,0,1:T(8,128)} reshape(f32[18,8,33,64]{2,1,3,0:T(8,128)} %copy.126) | data formatting | bytes 2433024 | tf_op jit(solution)/shard_map/jit(silu)/mul | solution.py:85
  79.9 3.4 %fusion.83 = (bf16[1,64,18,258]{3,1,2,0:T(8,128)(2,1)S(1)}, bf16[64,18,1,258]{3,0,1,2:T(8,128)(2,1)}, bf16[64,18,1,258]{3,0,1,2:T(8,128)(2,1)S(1)}, bf16[1,64,18,258]{3,1,2,0:T(8,128)(2,1)}) fusion(f32[18,258]{1,0:T(8,128)S(1)} %and_convert_fusion, f32[18,1,264,64]{2,3,0,1:T(8,128)} %reshape.212, f32[18,1,264,64]{2,3,0,1:T(8,128)S(1)} %reshape.213), kind=kLoop, calls=%fused_computation.124 | loop fusion | flops 1188864 | bytes 4774032 | tf_op jit(solution)/shard_map/convert_element_type | solution.py:85
  83.3 1.0 convolution_bitcast_fusion.3
  84.4 1.0 convolution_bitcast_fusion.4
  85.4 0.9 convolution_bitcast_fusion.5
  86.3 1.0 convolution_bitcast_fusion.6
  87.4 1.0 convolution_bitcast_fusion.7
  88.4 0.9 convolution_bitcast_fusion.8
  89.3 1.0 convolution_bitcast_fusion
  90.4 1.0 convolution_bitcast_fusion.1
  91.4 0.9 convolution_bitcast_fusion.2
  92.3 1.1 pad.6
  93.4 3.5 %reshape.217 = bf16[64,18,1,8,33]{4,3,0,1,2:T(8,128)(2,1)S(1)} reshape(bf16[64,18,1,264]{3,0,1,2:T(8,128)(2,1)} %pad.6) | data formatting | bytes 1216512 | tf_op jit(solution)/shard_map/conv_general_dilated | solution.py:22
  96.9 2.7 %copy.92 = bf16[64,18,1,8,33]{0,3,4,1,2:T(8,128)(2,1)} copy(bf16[64,18,1,8,33]{4,3,0,1,2:T(8,128)(2,1)S(1)} %reshape.217) | data formatting | bytes 1216512 | tf_op jit(solution)/shard_map/conv_general_dilated | solution.py:22
  99.6 0.9 slice.140
  100.5 2.9 %select_convert_fusion = bf16[16,8,33,64]{3,1,2,0:T(8,128)(2,1)S(1)} fusion(bf16[64,64,3,3]{1,0,3,2:T(8,128)(2,1)S(1)} %copy-done, bf16[64,18,1,7,2]{0,3,4,1,2:T(8,128)(2,1)S(1)} %slice.140, bf16[64,18,1,8,33]{0,3,4,1,2:T(8,128)(2,1)} %copy.92, pred[8,33]{0,1:T(8,128)(4,1)} %constant.49), kind=kOutput, calls=%fused_computation.9 | convolution fusion | flops 313903104 | bytes 1255176 | tf_op jit(solution)/shard_map/conv_general_dilated | solution.py:22
  103.8 2.2 copy.116
  106.0 1.0 pad.2
  107.0 3.5 %reshape.215 = bf16[64,18,1,8,33]{4,3,0,1,2:T(8,128)(2,1)S(1)} reshape(bf16[64,18,1,264]{3,0,1,2:T(8,128)(2,1)} %pad.2) | data formatting | bytes 1216512 | tf_op jit(solution)/shard_map/conv_general_dilated | solution.py:22
  110.5 2.7 %copy.83 = bf16[64,18,1,8,33]{0,3,4,1,2:T(8,128)(2,1)} copy(bf16[64,18,1,8,33]{4,3,0,1,2:T(8,128)(2,1)S(1)} %reshape.215) | data formatting | bytes 1216512 | tf_op jit(solution)/shard_map/conv_general_dilated | solution.py:22
  113.2 0.9 slice.135
  114.1 4.0 %select_convert_fusion.1 = bf16[16,8,33,64]{3,1,2,0:T(8,128)(2,1)S(1)} fusion(bf16[64,64,3,3]{1,0,3,2:T(8,128)(2,1)} %param.6, bf16[64,18,1,7,2]{0,3,4,1,2:T(8,128)(2,1)S(1)} %slice.135, bf16[64,18,1,8,33]{0,3,4,1,2:T(8,128)(2,1)} %copy.83, pred[8,33]{0,1:T(8,128)(4,1)} %constant.49), kind=kOutput, calls=%fused_computation.10 | convolution fusion | flops 313903104 | bytes 1255176 | tf_op jit(solution)/shard_map/conv_general_dilated | solution.py:22
  118.4 0.9 copy-done.1
  119.3 0.4 fusion.80
  119.9 0.7 pad_maximum_fusion.15
  120.6 0.6 fusion.37
  121.2 0.6 fusion.45
  121.8 0.3 fusion.41
  122.2 0.6 fusion.48
  122.8 0.6 fusion.55
  123.4 0.6 fusion.62
  124.0 0.6 fusion.73
  124.5 0.3 fusion.70
  124.9 0.7 pad_maximum_fusion.14
  125.9 2.2 copy.115
  128.0 126.1 %all-reduce.3.cloned.1.call-done = (f32[64,64,3,3]{1,0,3,2:T(8,128)}, f32[64,64,3,3]{1,0,3,2:T(8,128)}) async-done(((f32[64,64,3,3]{1,0,3,2:T(8,128)}, f32[64,64,3,3]{1,0,3,2:T(8,128)}), (f32[64,64,3,3]{1,0,3,2:T(8,128)}, f32[64,64,3,3]{1,0,3,2:T(8,128)})) %all-reduce.3.cloned.1.call-update) | async-done | bytes 294928 | tf_op jit(solution)/shard_map/psum | solution.py:94
  254.1 1.7 broadcast_multiply_fusion
  255.8 1.7 broadcast_multiply_fusion.1
  (70 shorter events, 1.9 us)
Async XLA Ops:
  7.2 45.3 %copy-start = (bf16[64,64,3,3]{1,0,3,2:T(8,128)(2,1)S(1)}, bf16[64,64,3,3]{1,0,3,2:T(8,128)(2,1)}, u32[]{:S(2)}) copy-start(bf16[64,64,3,3]{1,0,3,2:T(8,128)(2,1)} %param.5) | copy-start | bytes 221188
  7.2 246.9 %all-reduce.3.cloned.1.call-start = ((), (), s32[]{:S(2)}) async-start(), calls=%async_computation | async-start | bytes 1179648 | tf_op jit(solution)/shard_map/psum | solution.py:94
  9.7 7.6 %collective-permute-start = (bf16[1,128,2,256]{3,1,2,0:T(8,128)(2,1)S(1)}, bf16[1,128,2,256]{3,1,2,0:T(8,128)(2,1)S(1)}, u32[]{:S(2)}, u32[]{:S(2)}) collective-permute-start(bf16[1,128,2,256]{3,1,2,0:T(8,128)(2,1)S(1)} %get-tuple-element.22), channel_id=1, source_target_pairs={{0,4},{1,5},{2,6},{3,7},{8,12},{9,13},{10,14},{11,15},{16,20},{17,... | collective-permute-start | bytes 393224 | tf_op jit(solution)/shard_map/ppermute | solution.py:15
  14.6 6.9 %collective-permute-start.1 = (bf16[1,128,2,256]{3,1,2,0:T(8,128)(2,1)S(1)}, bf16[1,128,2,256]{3,1,2,0:T(8,128)(2,1)S(1)}, u32[]{:S(2)}, u32[]{:S(2)}) collective-permute-start(bf16[1,128,2,256]{3,1,2,0:T(8,128)(2,1)S(1)} %get-tuple-element.23), channel_id=1, source_target_pairs={{4,0},{5,1},{6,2},{7,3},{12,8},{13,9},{14,10},{15,11},{20,16},{21,... | collective-permute-start | bytes 393224 | tf_op jit(solution)/shard_map/ppermute | solution.py:16
  17.3 14.7 %copy-start.9 = (bf16[1,128,2,256]{3,1,2,0:T(8,128)(2,1)}, bf16[1,128,2,256]{3,1,2,0:T(8,128)(2,1)S(1)}, u32[]{:S(2)}) copy-start(bf16[1,128,2,256]{3,1,2,0:T(8,128)(2,1)S(1)} %collective-permute-done) | copy-start | bytes 393220
  21.4 10.5 %copy-start.11 = (bf16[1,128,2,256]{3,1,2,0:T(8,128)(2,1)}, bf16[1,128,2,256]{3,1,2,0:T(8,128)(2,1)S(1)}, u32[]{:S(2)}) copy-start(bf16[1,128,2,256]{3,1,2,0:T(8,128)(2,1)S(1)} %collective-permute-done.1) | copy-start | bytes 393220
  22.2 5.1 %collective-permute-start.2 = (bf16[1,128,20,2]{1,3,2,0:T(2,128)(2,1)S(1)}, bf16[1,128,20,2]{1,3,2,0:T(2,128)(2,1)S(1)}, u32[]{:S(2)}, u32[]{:S(2)}) collective-permute-start(bf16[1,128,20,2]{1,3,2,0:T(2,128)(2,1)S(1)} %copy.72), channel_id=1, source_target_pairs={{0,1},{1,2},{2,3},{4,5},{5,6},{6,7},{8,9},{9,10},{10,11},{12,13},{... | collective-permute-start | bytes 30728 | tf_op jit(solution)/shard_map/ppermute | solution.py:15
  26.0 5.6 %collective-permute-start.3 = (bf16[1,128,20,2]{1,3,2,0:T(2,128)(2,1)S(1)}, bf16[1,128,20,2]{1,3,2,0:T(2,128)(2,1)S(1)}, u32[]{:S(2)}, u32[]{:S(2)}) collective-permute-start(bf16[1,128,20,2]{1,3,2,0:T(2,128)(2,1)S(1)} %copy.73), channel_id=1, source_target_pairs={{1,0},{2,1},{3,2},{5,4},{6,5},{7,6},{9,8},{10,9},{11,10},{13,12},{... | collective-permute-start | bytes 30728 | tf_op jit(solution)/shard_map/ppermute | solution.py:16
  27.8 6.3 %copy-start.3 = (bf16[1,128,20,2]{3,1,2,0:T(8,128)(2,1)}, bf16[1,128,20,2]{3,1,2,0:T(8,128)(2,1)S(1)}, u32[]{:S(2)}) copy-start(bf16[1,128,20,2]{3,1,2,0:T(8,128)(2,1)S(1)} %copy.74) | copy-start | bytes 30724
  32.0 0.9 copy-start.5
  46.8 5.7 %copy-start.7 = (bf16[64,20,1,8,33]{0,3,4,1,2:T(8,128)(2,1)S(1)}, bf16[64,20,1,8,33]{0,3,4,1,2:T(8,128)(2,1)}, u32[]{:S(2)}) copy-start(bf16[64,20,1,8,33]{0,3,4,1,2:T(8,128)(2,1)} %copy.78) | copy-start | bytes 2027524
  46.8 5.7 %copy-start.25 = (pred[8,33]{0,1:T(8,128)(4,1)S(1)}, pred[8,33]{0,1:T(8,128)(4,1)}, u32[]{:S(2)}) copy-start(pred[8,33]{0,1:T(8,128)(4,1)} %constant.50) | copy-start | bytes 796
  52.5 4.5 %copy-start.8 = (bf16[64,20,1,8,33]{0,3,4,1,2:T(8,128)(2,1)S(1)}, bf16[64,20,1,8,33]{0,3,4,1,2:T(8,128)(2,1)}, u32[]{:S(2)}) copy-start(bf16[64,20,1,8,33]{0,3,4,1,2:T(8,128)(2,1)} %copy.87) | copy-start | bytes 2027524
  52.5 4.5 %copy-start.24 = (bf16[64,64,3,3]{1,0,3,2:T(8,128)(2,1)S(1)}, bf16[64,64,3,3]{1,0,3,2:T(8,128)(2,1)}, u32[]{:S(2)}) copy-start(bf16[64,64,3,3]{1,0,3,2:T(8,128)(2,1)} %param.6) | copy-start | bytes 221188
  79.9 3.4 %copy-start.13 = (bf16[1,64,16,256]{3,2,1,0:T(8,128)(2,1)S(1)}, bf16[1,64,16,256]{3,2,1,0:T(8,128)(2,1)}, u32[]{:S(2)}) copy-start(bf16[1,64,16,256]{3,2,1,0:T(8,128)(2,1)} %param.7) | copy-start | bytes 1572868
  103.6 2.4 copy-start.2
  114.1 4.3 %copy-start.14 = (bf16[1,64,16,256]{3,2,1,0:T(8,128)(2,1)S(1)}, bf16[1,64,16,256]{3,2,1,0:T(8,128)(2,1)}, u32[]{:S(2)}) copy-start(bf16[1,64,16,256]{3,2,1,0:T(8,128)(2,1)} %param.4) | copy-start | bytes 1572868
  118.2 1.2 copy-start.1
  118.2 1.6 copy-start.21
  118.2 1.6 copy-start.22
  118.2 1.6 copy-start.23
  118.2 1.6 copy-start.15
  118.2 1.6 copy-start.16
  118.2 1.6 copy-start.17
  118.2 1.6 copy-start.18
  118.2 1.6 copy-start.19
  118.2 1.6 copy-start.20
  118.3 2.4 copy-start.6
  118.3 2.4 copy-start.10
  118.3 2.4 copy-start.12
  119.8 1.5 copy-start.4
Sparse Core Ops, SparseCore 0:
  125.8 128.2 all-reduce.2
where the time goes:
time: 265 us; the launch traced here: 264 us
  waiting for transfers between devices  135 us (51%)
  local copies, waits for them, and re-layouts  64.7 us (24%)
  matrix products  28.8 us (11%)
  between operations  14.6 us (6%)
  starting transfers between devices  11 us (4%)
  other arithmetic  9.86 us (4%)
    psum x1, waiting for transfers between devices, on_device(): lax.psum((first_grad, second_grad), ('dp', 'row', 'col'))  126 us
    conv_general_dilated x12, local copies, waits for them, and re-layouts, convolve(): lax.conv_general_dilated(padded, kernel, (1, 1), 'VALID', dimension_numbe...  32.1 us
    conv_general_dilated x4, matrix products, convolve(): lax.conv_general_dilated(padded, kernel, (1, 1), 'VALID', dimension_numbe...  15.2 us
    dot_general x18, matrix products, kernel_grad(): jnp.einsum('nihw,nohw->oi', window, upstream, preferred_element_type=jnp....  13.6 us
    mul x2, local copies, waits for them, and re-layouts, on_device(): act_padded = (jax.nn.silu(hidden) * inside).astype(jnp.bfloat16)  10.1 us
    mul x2, local copies, waits for them, and re-layouts, on_device(): hid_padded = (act_grad * silu_grad(hidden) * inside).astype(jnp.bfloat16)  9 us
    ppermute x2, starting transfers between devices, extended(): before = lax.ppermute(last, axis, up)  8.36 us
    ppermute x2, waiting for transfers between devices, extended(): after = lax.ppermute(leading, axis, down)  7.89 us
  transfers between devices with their start and end apart: 5, of which 4 were waited for; matrix products, arithmetic and copies ran while one was open for 1% of the time, Pallas kernels for 0%

commit v1 on v0

--- a/solution.py
+++ b/solution.py
@@ -91,7 +91,7 @@
     hid_grad = hid_padded[:, :, 1:-1, 1:-1]
     input_grad = convolve(hid_padded, flipped(first_kernel)).astype(jnp.bfloat16)
     first_grad = kernel_grad(padded_in, hid_grad)
-    first_grad, second_grad = lax.psum((first_grad, second_grad), ("dp", "row", "col"))
+    first_grad, second_grad = lax.psum(lax.psum((first_grad, second_grad), ("row", "col")), "dp")
     return (outputs, input_grad, first_grad * factor, second_grad * factor)
 
 

time: 265 us -> 243 us (0.917)
  waiting for transfers between devices: 135 us -> 112 us
    psum x1 -> x2, waiting for transfers between devices: 126 us -> 103 us  [the longest x1 69.8 us: on_device(): lax.psum((first_grad, second_grad), ('row', 'col'))]
    unnamed x55 -> x41, local copies, waits for them, and re-layouts: 7.4 us -> 6.55 us
  transfers between devices with their start and end apart: 5 -> 6, of which waited for: 4 -> 5; matrix products, arithmetic and copies ran while one was open for 1% -> 2% of each run, Pallas kernels for 0% -> 0%
where the time goes in v1:
time: 243 us; the launch traced here: 242 us
  waiting for transfers between devices  112 us (46%)
  local copies, waits for them, and re-layouts  64 us (26%)
  matrix products  28.8 us (12%)
  between operations  14.5 us (6%)
  other arithmetic  11.6 us (5%)
  starting transfers between devices  11 us (5%)
    psum x1, waiting for transfers between devices, on_device(): lax.psum((first_grad, second_grad), ('row', 'col'))  69.8 us
    psum x1, waiting for transfers between devices, on_device(): lax.psum(lax.psum((first_grad, second_grad), ('row', 'col')), 'dp')  33 us
    conv_general_dilated x12, local copies, waits for them, and re-layouts, convolve(): lax.conv_general_dilated(padded, kernel, (1, 1), 'VALID', dimension_numbe...  32.3 us
    dot_general x18, matrix products, kernel_grad(): jnp.einsum('nihw,nohw->oi', window, upstream, preferred_element_type=jnp....  15 us
    conv_general_dilated x4, matrix products, convolve(): lax.conv_general_dilated(padded, kernel, (1, 1), 'VALID', dimension_numbe...  13.8 us
    mul x2, local copies, waits for them, and re-layouts, on_device(): act_padded = (jax.nn.silu(hidden) * inside).astype(jnp.bfloat16)  10.1 us
    mul x2, local copies, waits for them, and re-layouts, on_device(): hid_padded = (act_grad * silu_grad(hidden) * inside).astype(jnp.bfloat16)  9.01 us
    ppermute x2, starting transfers between devices, extended(): before = lax.ppermute(last, axis, up)  8.36 us
  transfers between devices with their start and end apart: 6, of which 5 were waited for; matrix products, arithmetic and copies ran while one was open for 2% of the time, Pallas kernels for 0%

profile of v1, /device:TPU:0, one launch (start us, length us, event | category | flops | bytes accessed | tf_op | source)
XLA Modules:
  0.0 242.0 jit_solution(17789860501502150041)
XLA Ops:
  7.2 1.2 copy_dynamic-update-slice_fusion.1
  8.5 1.2 copy_dynamic-update-slice_fusion
  9.7 4.9 %collective-permute-start = (bf16[1,128,2,256]{3,1,2,0:T(8,128)(2,1)S(1)}, bf16[1,128,2,256]{3,1,2,0:T(8,128)(2,1)S(1)}, u32[]{:S(2)}, u32[]{:S(2)}) collective-permute-start(bf16[1,128,2,256]{3,1,2,0:T(8,128)(2,1)S(1)} %get-tuple-element.24), channel_id=1, source_target_pairs={{0,4},{1,5},{2,6},{3,7},{8,12},{9,13},{10,14},{11,15},{16,20},{17,... | collective-permute-start | bytes 393224 | tf_op jit(solution)/shard_map/ppermute | solution.py:15
  14.6 1.3 collective-permute-start.1
  15.9 1.4 collective-permute-done
  17.3 4.1 %collective-permute-done.1 = bf16[1,128,2,256]{3,1,2,0:T(8,128)(2,1)S(1)} collective-permute-done((bf16[1,128,2,256]{3,1,2,0:T(8,128)(2,1)S(1)}, bf16[1,128,2,256]{3,1,2,0:T(8,128)(2,1)S(1)}, u32[]{:S(2)}, u32[]{:S(2)}) %collective-permute-start.1) | collective-permute-done | bytes 131104 | tf_op jit(solution)/shard_map/ppermute | solution.py:16
  21.6 0.3 fusion.118
  22.2 3.5 %collective-permute-start.2 = (bf16[1,128,20,2]{1,3,2,0:T(2,128)(2,1)S(1)}, bf16[1,128,20,2]{1,3,2,0:T(2,128)(2,1)S(1)}, u32[]{:S(2)}, u32[]{:S(2)}) collective-permute-start(bf16[1,128,20,2]{1,3,2,0:T(2,128)(2,1)S(1)} %copy.72), channel_id=1, source_target_pairs={{0,1},{1,2},{2,3},{4,5},{5,6},{6,7},{8,9},{9,10},{10,11},{12,13},{... | collective-permute-start | bytes 30728 | tf_op jit(solution)/shard_map/ppermute | solution.py:15
  26.0 1.3 collective-permute-start.3
  27.4 0.4 copy.74
  27.8 3.8 %collective-permute-done.3 = bf16[1,128,20,2]{1,3,2,0:T(2,128)(2,1)S(1)} collective-permute-done((bf16[1,128,20,2]{1,3,2,0:T(2,128)(2,1)S(1)}, bf16[1,128,20,2]{1,3,2,0:T(2,128)(2,1)S(1)}, u32[]{:S(2)}, u32[]{:S(2)}) %collective-permute-start.3) | collective-permute-done | bytes 10272 | tf_op jit(solution)/shard_map/ppermute | solution.py:16
  31.6 0.4 copy.75
  32.0 0.9 copy-done.5
  32.9 1.2 pad_maximum_fusion
  34.5 3.5 %reshape.214 = bf16[64,20,1,8,33]{4,3,0,1,2:T(8,128)(2,1)} reshape(bf16[64,20,1,264]{3,0,1,2:T(8,128)(2,1)S(1)} %pad) | data formatting | bytes 1351680 | tf_op jit(solution)/shard_map/conv_general_dilated | solution.py:22
  37.9 4.6 %copy.78 = bf16[64,20,1,8,33]{0,3,4,1,2:T(8,128)(2,1)} copy(bf16[64,20,1,8,33]{4,3,0,1,2:T(8,128)(2,1)} %reshape.214) | data formatting | bytes 1351680 | tf_op jit(solution)/shard_map/conv_general_dilated | solution.py:22
  42.6 0.9 slice.133
  43.6 3.3 %reshape.216 = bf16[64,20,1,8,33]{4,3,0,1,2:T(8,128)(2,1)} reshape(bf16[64,20,1,264]{3,0,1,2:T(8,128)(2,1)S(1)} %pad.4) | data formatting | bytes 1351680 | tf_op jit(solution)/shard_map/conv_general_dilated | solution.py:22
  46.9 4.7 %copy.87 = bf16[64,20,1,8,33]{0,3,4,1,2:T(8,128)(2,1)} copy(bf16[64,20,1,8,33]{4,3,0,1,2:T(8,128)(2,1)} %reshape.216) | data formatting | bytes 1351680 | tf_op jit(solution)/shard_map/conv_general_dilated | solution.py:22
  51.6 0.9 slice.138
  52.6 4.5 %fusion.4 = (f32[18,8,33,64]{3,1,2,0:T(8,128)}, f32[18,8,33,64]{3,1,2,0:T(8,128)S(1)}) fusion(pred[8,33]{0,1:T(8,128)(4,1)S(1)} %copy-done.18, bf16[64,64,3,3]{1,0,3,2:T(8,128)(2,1)S(1)} %copy-done, bf16[64,20,1,7,2]{0,3,4,1,2:T(8,128)(2,1)S(1)} %slice.133, bf16[64,20,1,8,33]{0,3,4,1,2:T(8,128)(2,1)S(1)} %copy-done.7), kind=kOutput, calls=%fused_computation.8 | convolution fusion | flops 354026496 | bytes 3218696 | tf_op jit(solution)/shard_map/conv_general_dilated | solution.py:22
  57.0 3.8 %select_multiply_fusion = f32[18,8,33,64]{3,1,2,0:T(8,128)} fusion(f32[18,8,33,64]{3,1,2,0:T(8,128)S(1)} %get-tuple-element.29, bf16[64,64,3,3]{1,0,3,2:T(8,128)(2,1)S(1)} %copy-done.15, bf16[64,20,1,7,2]{0,3,4,1,2:T(8,128)(2,1)S(1)} %slice.138, bf16[64,20,1,8,33]{0,3,4,1,2:T(8,128)(2,1)S(1)} %copy-done.8, pred[8,33]{0,1:T(8,128)(4,1)S(1)} %copy-done.18), kind=kOutput, calls=%fused_computation.6 | convolution fusion | flops 355547136 | bytes 3218696 | tf_op jit(solution)/shard_map/conv_general_dilated | solution.py:22
  60.8 5.2 %copy.127 = f32[18,8,33,64]{2,1,3,0:T(8,128)} copy(f32[18,8,33,64]{3,1,2,0:T(8,128)} %select_multiply_fusion) | data formatting | bytes 2433024 | tf_op jit(solution)/shard_map/mul | solution.py:90
  66.0 3.9 %reshape.213 = f32[18,1,264,64]{2,3,0,1:T(8,128)S(1)} reshape(f32[18,8,33,64]{2,1,3,0:T(8,128)} %copy.127) | data formatting | bytes 2433024 | tf_op jit(solution)/shard_map/mul | solution.py:90
  69.8 5.1 %copy.126 = f32[18,8,33,64]{2,1,3,0:T(8,128)} copy(f32[18,8,33,64]{3,1,2,0:T(8,128)} %get-tuple-element.28) | data formatting | bytes 2433024 | tf_op jit(solution)/shard_map/jit(silu)/mul | solution.py:85
  74.9 5.0 %reshape.212 = f32[18,1,264,64]{2,3,0,1:T(8,128)} reshape(f32[18,8,33,64]{2,1,3,0:T(8,128)} %copy.126) | data formatting | bytes 2433024 | tf_op jit(solution)/shard_map/jit(silu)/mul | solution.py:85
  79.9 3.5 %fusion.83 = (bf16[1,64,18,258]{3,1,2,0:T(8,128)(2,1)S(1)}, bf16[64,18,1,258]{3,0,1,2:T(8,128)(2,1)}, bf16[64,18,1,258]{3,0,1,2:T(8,128)(2,1)S(1)}, bf16[1,64,18,258]{3,1,2,0:T(8,128)(2,1)}) fusion(f32[18,258]{1,0:T(8,128)S(1)} %and_convert_fusion, f32[18,1,264,64]{2,3,0,1:T(8,128)} %reshape.212, f32[18,1,264,64]{2,3,0,1:T(8,128)S(1)} %reshape.213), kind=kLoop, calls=%fused_computation.124 | loop fusion | flops 1188864 | bytes 4774032 | tf_op jit(solution)/shard_map/convert_element_type | solution.py:85
  83.4 1.0 convolution_bitcast_fusion.3
  84.4 1.0 convolution_bitcast_fusion.4
  85.5 0.9 convolution_bitcast_fusion.5
  86.4 1.0 convolution_bitcast_fusion.6
  87.4 1.0 convolution_bitcast_fusion.7
  88.5 1.0 convolution_bitcast_fusion.8
  89.4 1.0 convolution_bitcast_fusion
  90.5 1.0 convolution_bitcast_fusion.1
  91.5 0.9 convolution_bitcast_fusion.2
  92.5 1.0 pad.6
  93.5 3.5 %reshape.217 = bf16[64,18,1,8,33]{4,3,0,1,2:T(8,128)(2,1)S(1)} reshape(bf16[64,18,1,264]{3,0,1,2:T(8,128)(2,1)} %pad.6) | data formatting | bytes 1216512 | tf_op jit(solution)/shard_map/conv_general_dilated | solution.py:22
  97.0 2.7 %copy.92 = bf16[64,18,1,8,33]{0,3,4,1,2:T(8,128)(2,1)} copy(bf16[64,18,1,8,33]{4,3,0,1,2:T(8,128)(2,1)S(1)} %reshape.217) | data formatting | bytes 1216512 | tf_op jit(solution)/shard_map/conv_general_dilated | solution.py:22
  99.7 0.9 slice.140
  100.6 2.9 %select_convert_fusion = bf16[16,8,33,64]{3,1,2,0:T(8,128)(2,1)S(1)} fusion(bf16[64,64,3,3]{1,0,3,2:T(8,128)(2,1)S(1)} %copy-done, bf16[64,18,1,7,2]{0,3,4,1,2:T(8,128)(2,1)S(1)} %slice.140, bf16[64,18,1,8,33]{0,3,4,1,2:T(8,128)(2,1)} %copy.92, pred[8,33]{0,1:T(8,128)(4,1)} %constant.49), kind=kOutput, calls=%fused_computation.9 | convolution fusion | flops 313903104 | bytes 1255176 | tf_op jit(solution)/shard_map/conv_general_dilated | solution.py:22
  103.9 2.2 copy.116
  106.0 1.0 pad.2
  107.1 3.5 %reshape.215 = bf16[64,18,1,8,33]{4,3,0,1,2:T(8,128)(2,1)S(1)} reshape(bf16[64,18,1,264]{3,0,1,2:T(8,128)(2,1)} %pad.2) | data formatting | bytes 1216512 | tf_op jit(solution)/shard_map/conv_general_dilated | solution.py:22
  110.6 2.7 %copy.83 = bf16[64,18,1,8,33]{0,3,4,1,2:T(8,128)(2,1)} copy(bf16[64,18,1,8,33]{4,3,0,1,2:T(8,128)(2,1)S(1)} %reshape.215) | data formatting | bytes 1216512 | tf_op jit(solution)/shard_map/conv_general_dilated | solution.py:22
  113.3 1.0 slice.135
  114.4 1.7 fusion.80
  116.1 0.9 maximum_bitcast_fusion.13
  117.0 0.9 maximum_bitcast_fusion.11
  117.8 0.7 pad_maximum_fusion.15
  118.6 0.6 fusion.37
  119.2 0.6 fusion.45
  120.1 0.6 fusion.48
  120.7 0.6 fusion.55
  121.3 0.6 fusion.62
  121.9 0.6 fusion.73
  122.5 0.3 fusion.70
  122.9 0.7 pad_maximum_fusion.14
  123.7 2.7 %select_convert_fusion.1 = bf16[16,8,33,64]{3,1,2,0:T(8,128)(2,1)S(1)} fusion(bf16[64,64,3,3]{1,0,3,2:T(8,128)(2,1)S(1)} %copy-done.16, bf16[64,18,1,7,2]{0,3,4,1,2:T(8,128)(2,1)S(1)} %slice.135, bf16[64,18,1,8,33]{0,3,4,1,2:T(8,128)(2,1)S(1)} %copy-done.9, pred[8,33]{0,1:T(8,128)(4,1)S(1)} %copy-done.17), kind=kOutput, calls=%fused_computation.10 | convolution fusion | flops 313903104 | bytes 1255176 | tf_op jit(solution)/shard_map/conv_general_dilated | solution.py:22
  126.6 69.8 %all-reduce.5.cloned.1.call-done = (f32[64,64,3,3]{1,0,3,2:T(8,128)}, f32[64,64,3,3]{1,0,3,2:T(8,128)}) async-done(((f32[64,64,3,3]{1,0,3,2:T(8,128)}, f32[64,64,3,3]{1,0,3,2:T(8,128)}), (f32[64,64,3,3]{1,0,3,2:T(8,128)}, f32[64,64,3,3]{1,0,3,2:T(8,128)})) %all-reduce.5.cloned.1.call-update) | async-done | bytes 294928 | tf_op jit(solution)/shard_map/psum | solution.py:94
  196.6 2.2 copy.115
  198.7 33.0 %all-reduce.7.cloned.1.call-done = (f32[64,64,3,3]{1,0,3,2:T(8,128)}, f32[64,64,3,3]{1,0,3,2:T(8,128)}) async-done(((f32[64,64,3,3]{1,0,3,2:T(8,128)}, f32[64,64,3,3]{1,0,3,2:T(8,128)}), (f32[64,64,3,3]{1,0,3,2:T(8,128)}, f32[64,64,3,3]{1,0,3,2:T(8,128)})) %all-reduce.7.cloned.1.call-update) | async-done | bytes 294928 | tf_op jit(solution)/shard_map/psum | solution.py:94
  231.7 1.7 broadcast_multiply_fusion
  233.4 1.7 broadcast_multiply_fusion.1
  (59 shorter events, 2.5 us)
Async XLA Ops:
  7.2 45.4 %copy-start = (bf16[64,64,3,3]{1,0,3,2:T(8,128)(2,1)S(1)}, bf16[64,64,3,3]{1,0,3,2:T(8,128)(2,1)}, u32[]{:S(2)}) copy-start(bf16[64,64,3,3]{1,0,3,2:T(8,128)(2,1)} %param.5) | copy-start | bytes 221188
  7.2 189.2 %all-reduce.5.cloned.1.call-start = ((), (), s32[]{:S(2)}) async-start(), calls=%async_computation | async-start | bytes 1179648 | tf_op jit(solution)/shard_map/psum | solution.py:94
  9.7 7.6 %collective-permute-start = (bf16[1,128,2,256]{3,1,2,0:T(8,128)(2,1)S(1)}, bf16[1,128,2,256]{3,1,2,0:T(8,128)(2,1)S(1)}, u32[]{:S(2)}, u32[]{:S(2)}) collective-permute-start(bf16[1,128,2,256]{3,1,2,0:T(8,128)(2,1)S(1)} %get-tuple-element.24), channel_id=1, source_target_pairs={{0,4},{1,5},{2,6},{3,7},{8,12},{9,13},{10,14},{11,15},{16,20},{17,... | collective-permute-start | bytes 393224 | tf_op jit(solution)/shard_map/ppermute | solution.py:15
  14.6 6.9 %collective-permute-start.1 = (bf16[1,128,2,256]{3,1,2,0:T(8,128)(2,1)S(1)}, bf16[1,128,2,256]{3,1,2,0:T(8,128)(2,1)S(1)}, u32[]{:S(2)}, u32[]{:S(2)}) collective-permute-start(bf16[1,128,2,256]{3,1,2,0:T(8,128)(2,1)S(1)} %get-tuple-element.25), channel_id=1, source_target_pairs={{4,0},{5,1},{6,2},{7,3},{12,8},{13,9},{14,10},{15,11},{20,16},{21,... | collective-permute-start | bytes 393224 | tf_op jit(solution)/shard_map/ppermute | solution.py:16
  17.3 14.7 %copy-start.10 = (bf16[1,128,2,256]{3,1,2,0:T(8,128)(2,1)}, bf16[1,128,2,256]{3,1,2,0:T(8,128)(2,1)S(1)}, u32[]{:S(2)}) copy-start(bf16[1,128,2,256]{3,1,2,0:T(8,128)(2,1)S(1)} %collective-permute-done) | copy-start | bytes 393220
  21.4 10.5 %copy-start.12 = (bf16[1,128,2,256]{3,1,2,0:T(8,128)(2,1)}, bf16[1,128,2,256]{3,1,2,0:T(8,128)(2,1)S(1)}, u32[]{:S(2)}) copy-start(bf16[1,128,2,256]{3,1,2,0:T(8,128)(2,1)S(1)} %collective-permute-done.1) | copy-start | bytes 393220
  22.2 5.1 %collective-permute-start.2 = (bf16[1,128,20,2]{1,3,2,0:T(2,128)(2,1)S(1)}, bf16[1,128,20,2]{1,3,2,0:T(2,128)(2,1)S(1)}, u32[]{:S(2)}, u32[]{:S(2)}) collective-permute-start(bf16[1,128,20,2]{1,3,2,0:T(2,128)(2,1)S(1)} %copy.72), channel_id=1, source_target_pairs={{0,1},{1,2},{2,3},{4,5},{5,6},{6,7},{8,9},{9,10},{10,11},{12,13},{... | collective-permute-start | bytes 30728 | tf_op jit(solution)/shard_map/ppermute | solution.py:15
  26.0 5.6 %collective-permute-start.3 = (bf16[1,128,20,2]{1,3,2,0:T(2,128)(2,1)S(1)}, bf16[1,128,20,2]{1,3,2,0:T(2,128)(2,1)S(1)}, u32[]{:S(2)}, u32[]{:S(2)}) collective-permute-start(bf16[1,128,20,2]{1,3,2,0:T(2,128)(2,1)S(1)} %copy.73), channel_id=1, source_target_pairs={{1,0},{2,1},{3,2},{5,4},{6,5},{7,6},{9,8},{10,9},{11,10},{13,12},{... | collective-permute-start | bytes 30728 | tf_op jit(solution)/shard_map/ppermute | solution.py:16
  27.8 6.3 %copy-start.3 = (bf16[1,128,20,2]{3,1,2,0:T(8,128)(2,1)}, bf16[1,128,20,2]{3,1,2,0:T(8,128)(2,1)S(1)}, u32[]{:S(2)}) copy-start(bf16[1,128,20,2]{3,1,2,0:T(8,128)(2,1)S(1)} %copy.74) | copy-start | bytes 30724
  32.0 0.9 copy-start.5
  46.9 5.7 %copy-start.7 = (bf16[64,20,1,8,33]{0,3,4,1,2:T(8,128)(2,1)S(1)}, bf16[64,20,1,8,33]{0,3,4,1,2:T(8,128)(2,1)}, u32[]{:S(2)}) copy-start(bf16[64,20,1,8,33]{0,3,4,1,2:T(8,128)(2,1)} %copy.78) | copy-start | bytes 2027524
  46.9 5.7 %copy-start.18 = (pred[8,33]{0,1:T(8,128)(4,1)S(1)}, pred[8,33]{0,1:T(8,128)(4,1)}, u32[]{:S(2)}) copy-start(pred[8,33]{0,1:T(8,128)(4,1)} %constant.50) | copy-start | bytes 796
  52.5 4.5 %copy-start.8 = (bf16[64,20,1,8,33]{0,3,4,1,2:T(8,128)(2,1)S(1)}, bf16[64,20,1,8,33]{0,3,4,1,2:T(8,128)(2,1)}, u32[]{:S(2)}) copy-start(bf16[64,20,1,8,33]{0,3,4,1,2:T(8,128)(2,1)} %copy.87) | copy-start | bytes 2027524
  52.6 4.5 %copy-start.15 = (bf16[64,64,3,3]{1,0,3,2:T(8,128)(2,1)S(1)}, bf16[64,64,3,3]{1,0,3,2:T(8,128)(2,1)}, u32[]{:S(2)}) copy-start(bf16[64,64,3,3]{1,0,3,2:T(8,128)(2,1)} %param.6) | copy-start | bytes 221188
  79.9 3.5 %copy-start.14 = (bf16[1,64,16,256]{3,2,1,0:T(8,128)(2,1)S(1)}, bf16[1,64,16,256]{3,2,1,0:T(8,128)(2,1)}, u32[]{:S(2)}) copy-start(bf16[1,64,16,256]{3,2,1,0:T(8,128)(2,1)} %param.7) | copy-start | bytes 1572868
  103.7 2.4 copy-start.2
  113.3 5.3 %copy-start.1 = (bf16[1,64,18,258]{3,1,2,0:T(8,128)(2,1)S(1)}, bf16[1,64,18,258]{3,1,2,0:T(8,128)(2,1)}, u32[]{:S(2)}) copy-start(bf16[1,64,18,258]{3,1,2,0:T(8,128)(2,1)} %get-tuple-element.27) | copy-start | bytes 1783300
  113.3 5.3 %copy-start.6 = (bf16[1,128,20,2]{3,1,2,0:T(8,128)(2,1)S(1)}, bf16[1,128,20,2]{3,1,2,0:T(8,128)(2,1)}, u32[]{:S(2)}) copy-start(bf16[1,128,20,2]{3,1,2,0:T(8,128)(2,1)} %copy-done.5) | copy-start | bytes 30724
  113.3 5.3 %copy-start.11 = (bf16[1,128,2,256]{3,1,2,0:T(8,128)(2,1)S(1)}, bf16[1,128,2,256]{3,1,2,0:T(8,128)(2,1)}, u32[]{:S(2)}) copy-start(bf16[1,128,2,256]{3,1,2,0:T(8,128)(2,1)} %copy-done.10) | copy-start | bytes 393220
  113.3 5.3 %copy-start.13 = (bf16[1,128,2,256]{3,1,2,0:T(8,128)(2,1)S(1)}, bf16[1,128,2,256]{3,1,2,0:T(8,128)(2,1)}, u32[]{:S(2)}) copy-start(bf16[1,128,2,256]{3,1,2,0:T(8,128)(2,1)} %copy-done.12) | copy-start | bytes 393220
  116.1 3.1 %copy-start.4 = (bf16[1,128,20,2]{3,1,2,0:T(8,128)(2,1)S(1)}, bf16[1,128,20,2]{3,1,2,0:T(8,128)(2,1)}, u32[]{:S(2)}) copy-start(bf16[1,128,20,2]{3,1,2,0:T(8,128)(2,1)} %copy-done.3) | copy-start | bytes 30724
  122.4 1.3 copy-start.9
  122.5 1.3 copy-start.16
  122.5 1.3 copy-start.17
  123.6 108.1 %all-reduce.7.cloned.1.call-start = ((), (), s32[]{:S(2)}) async-start(), calls=%async_computation.1 | async-start | bytes 1179648 | tf_op jit(solution)/shard_map/psum | solution.py:94
Sparse Core Ops, SparseCore 0:
  123.7 72.5 all-reduce.4
  198.7 32.9 all-reduce.6
